TPU v7x, 128 devices: a whole 4x4x4 slice. The times are simulated.
128 devices in a mesh: lat: 32 (over z, y, x_hi), lev: 4 (over x_lo, core).
Axes of the slice: x: 4 (x_hi: 2, x_lo: 2; x = x_hi * 2 + x_lo), y: 4, z: 4, core: 2. Of those that a mesh axis runs over, the one named last changes fastest.
Arguments:
- spec_in: bfloat16 [192, 171, 4, 512], P('lat', None, None, 'lev'), may hold values from -6 to 6
- cotangent: bfloat16 [192, 171, 4, 512], P('lat', None, None, 'lev'), may hold values from -6 to 6
- legendre: bfloat16 [192, 171, 256], P('lat'), may hold values from -0.4375 to 0.4375
- quad_weights: float32 [256], replicated, may hold values from 0.5 to 2
- wave_order: int32 [192], replicated, may hold values from 0 to 191, each once
- norm_gain: float32 [256], replicated, may hold values from 0.5 to 1.5
- weight_in: bfloat16 [256, 512], replicated, may hold values from -0.375 to 0.375
- bias_in: float32 [512], replicated, may hold values from -3 to 3
- weight_mid: bfloat16 [512, 512], replicated, may hold values from -0.25 to 0.25
- bias_mid: float32 [512], replicated, may hold values from -3 to 3
- weight_out: bfloat16 [512, 256], replicated, may hold values from -0.25 to 0.25
Outputs:
- grad_spec: float32 [192, 171, 4, 512], P('lat', None, None, 'lev')
- grad_gain: float32 [256], replicated
- grad_w_in: float32 [256, 512], replicated
- grad_b_in: float32 [512], replicated
- grad_w_mid: float32 [512, 512], replicated
- grad_b_mid: float32 [512], replicated
- grad_w_out: float32 [512, 256], replicated
Inputs may be any that keep to these rules, and one draw needn't show every extreme that they name: `wave_order`: each of 0 to 191 appears once; a slot holding 171 or more is unused.
All inputs are finite; a program needn't handle non-finite values.
Results may differ from a plain program's by a relative error of at most 0.007.
Values may be sent and summed in bfloat16 or wider, within the bound.
A program may use at most 128 MiB of HBM per device.

v0:
```python
import math
import jax
import jax.numpy as jnp
from jax import lax
from jax.sharding import PartitionSpec as P

WAVES = 171
NLAT = 256
NLON = 512
MEMBERS = 4
time_step = 0.5
norm_eps = 1e-06


def in_one_piece(arrays, axis, split_dim, concat_dim, along):
    ends, at = ([], 0)
    for a in arrays[:-1]:
        at += a.shape[along]
        ends.append(at)
    both = jnp.concatenate(arrays, axis=along)
    return tuple(
        jnp.split(
            lax.all_to_all(both, axis, split_axis=split_dim, concat_axis=concat_dim, tiled=True),
            ends,
            axis=along,
        )
    )


def spectral_masks(waves_held, degree_count):
    degree = jnp.arange(degree_count, dtype=jnp.int32)
    living = (waves_held[:, None] <= degree[None, :]) & (waves_held[:, None] < WAVES)
    ratio = (degree * (degree + 1)).astype(jnp.float32) / float(WAVES * (WAVES - 1))
    factor = 1.0 / (1.0 + ratio * ratio)
    shrink = jnp.where(living, factor[None, :], jnp.zeros_like(factor)[None, :])
    return (living, shrink)


def fourier_table(waves_all):
    longitude = jnp.arange(NLON, dtype=jnp.int32)
    phase_steps = waves_all[:, None] * longitude[None, :] % NLON
    angles = phase_steps.astype(jnp.float32) * (2.0 * math.pi / NLON)
    weight_scale = jnp.where(waves_all < WAVES, math.sqrt(2.0 / NLON), 0.0).astype(jnp.float32)[
        :, None
    ]
    return jnp.stack(
        [jnp.cos(angles) * weight_scale, -jnp.sin(angles) * weight_scale], axis=1
    ).astype(jnp.bfloat16)


def contract_rows(left, right):
    return lax.dot_general(
        left, right, (((0,), (0,)), ((), ())), preferred_element_type=jnp.float32
    )


def contract_cols(left, right):
    return lax.dot_general(
        left, right, (((1,), (1,)), ((), ())), preferred_element_type=jnp.float32
    )


def column_grads(
    columns, column_cot, norm_gain, weight_in, bias_in, weight_mid, bias_mid, weight_out
):
    inputs = columns.astype(jnp.float32)
    inverse = lax.rsqrt(jnp.mean(inputs * inputs, axis=1, keepdims=True) + norm_eps)
    normed = (inputs * inverse * norm_gain).astype(jnp.bfloat16)
    pre_one = jnp.dot(normed, weight_in, preferred_element_type=jnp.float32) + bias_in
    sig_one = jax.nn.sigmoid(pre_one)
    act_one = (pre_one * sig_one).astype(jnp.bfloat16)
    pre_two = jnp.dot(act_one, weight_mid, preferred_element_type=jnp.float32) + bias_mid
    sig_two = jax.nn.sigmoid(pre_two)
    act_two = (pre_two * sig_two).astype(jnp.bfloat16)
    gradient_third = contract_rows(act_two, column_cot)
    back_two = contract_cols(column_cot, weight_out)
    delta_two = (back_two * sig_two * (1.0 + pre_two * (1.0 - sig_two))).astype(jnp.bfloat16)
    gradient_second = contract_rows(act_one, delta_two)
    offset_second = jnp.sum(delta_two.astype(jnp.float32), axis=0)
    back_one = contract_cols(delta_two, weight_mid)
    delta_one = (back_one * sig_one * (1.0 + pre_one * (1.0 - sig_one))).astype(jnp.bfloat16)
    gradient_first = contract_rows(normed, delta_one)
    offset_first = jnp.sum(delta_one.astype(jnp.float32), axis=0)
    back_norm = contract_cols(delta_one, weight_in)
    gradient_gain = jnp.sum(back_norm * inputs * inverse, axis=0)
    scaled = back_norm * norm_gain
    grad_columns = inverse * scaled - inputs * inverse * inverse * inverse * jnp.mean(
        scaled * inputs, axis=1, keepdims=True
    )
    return (
        grad_columns.astype(jnp.bfloat16),
        (
            gradient_gain,
            gradient_first,
            offset_first,
            gradient_second,
            offset_second,
            gradient_third,
        ),
    )


def synthesize(wave_table, coeffs):
    shape = coeffs.shape
    split = coeffs.reshape(shape[0], shape[1], shape[2], shape[3] // 2, 2)
    return jnp.einsum(
        "spo,stecp->otec", wave_table, split, preferred_element_type=jnp.float32
    ).astype(jnp.bfloat16)


def analyze(wave_table, values):
    result = jnp.einsum(
        "spo,otec->stecp", wave_table, values, preferred_element_type=jnp.float32
    ).astype(jnp.bfloat16)
    shape = result.shape
    return result.reshape(shape[0], shape[1], shape[2], shape[3] * 2)


def local(
    spec_in,
    cotangent,
    legendre,
    quad_weights,
    wave_order,
    norm_gain,
    weight_in,
    bias_in,
    weight_mid,
    bias_mid,
    weight_out,
):
    slots_here = spec_in.shape[0]
    own_waves = lax.dynamic_slice_in_dim(wave_order, lax.axis_index("lat") * slots_here, slots_here)
    living, shrink = spectral_masks(own_waves, spec_in.shape[1])
    basis_rows = jnp.where(living[:, :, None], legendre, jnp.zeros_like(legendre))
    wave_table = fourier_table(wave_order)
    fourier = jnp.einsum(
        "slt,slek->stek", basis_rows, spec_in, preferred_element_type=jnp.float32
    ).astype(jnp.bfloat16)
    pushed = (time_step * cotangent.astype(jnp.float32) * shrink[:, :, None, None]).astype(
        jnp.bfloat16
    )
    pulled = jnp.einsum("slt,slek->stek", basis_rows, pushed, preferred_element_type=jnp.float32)
    pulled = (quad_weights[None, :, None, None] * pulled).astype(jnp.bfloat16)
    fourier_all, pulled_all = in_one_piece((fourier, pulled), "lat", 1, 0, 2)
    grid_part = synthesize(wave_table, fourier_all)
    cot_part = synthesize(wave_table, pulled_all)
    grid_values, grid_cot = in_one_piece((grid_part, cot_part), "lev", 0, 3, 1)
    grid_shape = grid_values.shape
    grad_rows, grads_local = column_grads(
        grid_values.reshape(-1, grid_shape[3]),
        grid_cot.reshape(-1, grid_shape[3]),
        norm_gain,
        weight_in,
        bias_in,
        weight_mid,
        bias_mid,
        weight_out,
    )
    grad_grid = grad_rows.reshape(grid_shape)
    grad_part = lax.all_to_all(grad_grid, "lev", split_axis=3, concat_axis=0, tiled=True)
    back_fourier = analyze(wave_table, grad_part)
    back_slots = lax.all_to_all(back_fourier, "lat", split_axis=0, concat_axis=1, tiled=True)
    summed = lax.psum(
        (
            grads_local[0],
            grads_local[1],
            grads_local[2],
            grads_local[3],
            grads_local[4],
            grads_local[5],
        ),
        ("lat", "lev"),
    )
    factor = float(MEMBERS * NLAT * NLON) ** (-0.5)
    grads = tuple((piece * factor for piece in summed))
    grad_spec = cotangent.astype(jnp.float32) * shrink[:, :, None, None] + jnp.einsum(
        "slt,stek->slek", basis_rows, back_slots, preferred_element_type=jnp.float32
    )
    return (grad_spec, grads[0], grads[1], grads[2], grads[3], grads[4], grads[5])


def solution(mesh):
    placed = (
        P("lat", None, None, "lev"),
        P("lat", None, None, "lev"),
        P("lat", None, None),
        P(),
        P(),
        P(),
        P(),
        P(),
        P(),
        P(),
        P(),
    )
    return jax.shard_map(
        local,
        mesh=mesh,
        in_specs=placed,
        out_specs=(P("lat", None, None, "lev"), P(), P(), P(), P(), P(), P()),
        check_vma=False,
    )
```

profile of v0, /device:TPU:1, one launch (start us, length us, event | category | flops | bytes accessed | tf_op | source)
XLA Modules:
  0.0 443.2 jit_solution(5164331908292639618)
XLA Ops:
  7.2 0.0 copy-start
  7.2 0.8 broadcast_compare_fusion
  8.0 0.1 fusion.29
  8.1 0.7 broadcast_select_fusion.4
  8.8 1.9 convolution_convert_fusion
  10.7 2.4 multiply_convert_fusion.6
  13.2 0.3 pad_maximum_fusion.1
  13.5 3.7 copy.95
  17.2 12.1 %all-to-all-start = ((bf16[6,256,8,128]{3,2,0,1:T(8,128)(2,1)}), bf16[6,256,8,128]{3,2,0,1:T(8,128)(2,1)}, u32[]{:S(2)}, u32[]{:S(2)}) async-start(bf16[6,256,8,128]{3,2,0,1:T(8,128)(2,1)} %copy.95), calls=%async_computation | async-start | bytes 6291456 | tf_op jit(solution)/shard_map/all_to_all | solution.py:23
  29.3 1.9 multiply_convert_fusion.8
  31.2 38.7 %all-to-all-done = bf16[6,256,8,128]{3,2,0,1:T(8,128)(2,1)} async-done(((bf16[6,256,8,128]{3,2,0,1:T(8,128)(2,1)}), bf16[6,256,8,128]{3,2,0,1:T(8,128)(2,1)}, u32[]{:S(2)}, u32[]{:S(2)}) %all-to-all-start) | async-done | bytes 3145760 | tf_op jit(solution)/shard_map/all_to_all | solution.py:23
  69.9 2.7 copy.97
  72.7 2.2 fusion.45
  74.9 5.3 %copy.98 = bf16[192,8,4,128]{0,1,3,2:T(8,128)(2,1)} copy(bf16[192,8,4,128]{3,2,1,0:T(4,128)(2,1)} %get-tuple-element.61) | data formatting | bytes 3145728 | tf_op jit(solution)/shard_map/split | solution.py:22
  80.2 4.2 copy.100
  84.4 3.7 bitcast_convert_fusion.1
  88.2 2.1 bitcast_convert_fusion
  90.2 2.3 pad_maximum_fusion
  92.6 13.8 %copy.102 = bf16[512,16,4,64]{3,2,1,0:T(4,128)(2,1)} copy(bf16[512,16,4,64]{0,3,2,1:T(8,128)(2,1)} %pad_maximum_fusion) | data formatting | bytes 8388608 | tf_op jit(solution)/shard_map/concatenate | solution.py:20
  106.4 9.5 %reshape.301 = bf16[4,2,262144]{2,1,0:T(2,128)(2,1)} reshape(bf16[512,16,4,64]{3,2,1,0:T(4,128)(2,1)} %copy.102) | data formatting | bytes 8388608
  115.9 55.2 %all_to_all.72 = bf16[4,2,262144]{2,1,0:T(2,128)(2,1)} all-to-all(bf16[4,2,262144]{2,1,0:T(2,128)(2,1)} %reshape.301), channel_id=1, replica_groups=mesh['lat'=32,'lev'=4] {'lev'}, dimensions={0} | all-to-all | bytes 8388608 | tf_op jit(solution)/shard_map/all_to_all | solution.py:23
  171.1 9.3 %reshape.302 = bf16[512,16,4,64]{3,2,1,0:T(4,128)(2,1)} reshape(bf16[4,2,262144]{2,1,0:T(2,128)(2,1)} %all_to_all.72) | data formatting | bytes 8388608
  180.4 12.7 %copy.104 = bf16[128,16,4,4,64]{0,4,3,2,1:T(8,128)(2,1)} copy(bf16[128,16,4,4,64]{4,2,1,0,3:T(4,128)(2,1)} %bitcast.65) | data formatting | bytes 8388608 | tf_op jit(solution)/shard_map/all_to_all | solution.py:23
  193.1 2.0 multiply_reduce_fusion.2
  195.1 4.7 %fusion.44 = (bf16[128,8,4,256]{0,3,2,1:T(8,128)(2,1)S(1)}, f32[128,8,4,256]{0,3,2,1:T(8,128)}) fusion(bf16[128,16,4,256]{0,3,2,1:T(8,128)(2,1)} %bitcast.67), kind=kLoop, calls=%fused_computation.85 | loop fusion | flops 1048576 | bytes 10485760 | tf_op jit(solution)/shard_map/split | solution.py:22
  199.8 0.3 copy.106
  200.1 0.3 rsqrt.12
  200.4 2.9 copy.107
  203.2 2.5 reshape.291
  205.8 6.3 %copy.108 = f32[128,8,4,256]{3,2,1,0:T(4,128)} copy(f32[128,8,4,256]{0,3,2,1:T(8,128)} %get-tuple-element.60) | data formatting | bytes 8388608 | tf_op jit(solution)/shard_map/convert_element_type | solution.py:66
  212.1 5.4 %reshape.294 = f32[4096,256]{1,0:T(8,128)} reshape(f32[128,8,4,256]{3,2,1,0:T(4,128)} %copy.108) | data formatting | bytes 8388608 | tf_op jit(solution)/shard_map/convert_element_type | solution.py:66
  217.5 0.0 copy-start.9
  217.5 4.9 %multiply_convert_fusion.3 = (bf16[4096,512]{1,0:T(8,128)(2,1)S(1)}, f32[4096,512]{1,0:T(8,128)S(1)}) fusion(f32[512]{0:T(512)S(1)} %copy-done.17, bf16[256,512]{1,0:T(8,128)(2,1)S(1)} %copy-done.10, f32[4096,256]{1,0:T(8,128)} %reshape.294, f32[256]{0:T(256)S(1)} %copy-done.14, f32[4096]{0:T(1024)S(1)} %rsqrt.12), kind=kOutput, calls=%fused_computation.6 | convolution fusion | flops 1089470464 | bytes 17058816 | tf_op jit(solution)/shard_map/dot_general | solution.py:69
  222.4 0.0 copy-start.16
  222.4 2.4 fusion.46
  224.9 3.9 convert_reduce_fusion
  228.8 3.3 fusion.47
  232.1 4.4 %convert_reduce_fusion.1 = (f32[512]{0:T(512)S(1)}, bf16[4096,512]{1,0:T(8,128)(2,1)S(1)}) fusion(f32[4096,512]{1,0:T(8,128)S(1)} %get-tuple-element.68, f32[512]{0:T(512)S(1)} %copy-done.17, bf16[4096,512]{1,0:T(8,128)(2,1)S(1)} %get-tuple-element.73, bf16[512,512]{1,0:T(8,128)(2,1)S(1)} %copy-done.9), kind=kOutput, calls=%fused_computation.2 | convolution fusion | flops 2172648960 | bytes 17305600 | tf_op jit(solution)/shard_map/dot_general | solution.py:58
  236.6 1.9 multiply_reduce_fusion
  238.5 0.1 copy-done.3
  238.5 3.2 subtract_convert_fusion
  241.7 2.5 reshape.292
  244.3 4.1 copy.109
  248.4 4.7 %all-to-all-start.2 = ((bf16[128,8,4,256]{0,2,1,3:T(4,128)(2,1)}), bf16[128,8,4,256]{0,2,1,3:T(4,128)(2,1)S(1)}, u32[]{:S(2)}, u32[]{:S(2)}) async-start(bf16[128,8,4,256]{0,2,1,3:T(4,128)(2,1)} %copy.109), calls=%async_computation.2 | async-start | bytes 4194304 | tf_op jit(solution)/shard_map/all_to_all | solution.py:161
  253.0 6.9 %fusion.42 = f32[256,512]{1,0:T(8,128)} fusion(bf16[4096,512]{1,0:T(8,128)(2,1)} %copy-done.3, f32[4096,256]{1,0:T(8,128)} %reshape.294, f32[256]{0:T(256)S(1)} %copy-done.14, f32[4096]{0:T(1024)S(1)} %rsqrt.12), kind=kOutput, calls=%fused_computation.83 | convolution fusion | flops 1076887552 | bytes 8930304 | tf_op jit(solution)/shard_map/dot_general | solution.py:52
  259.9 6.6 %fusion = f32[512,256]{1,0:T(8,128)} fusion(bf16[4096,256]{1,0:T(8,128)(2,1)S(1)} %copy-done.8, f32[4096,512]{1,0:T(8,128)} %copy-done.4, f32[512]{0:T(512)S(1)} %copy-done.18), kind=kOutput, calls=%fused_computation.16 | convolution fusion | flops 1086324736 | bytes 11012096 | tf_op jit(solution)/shard_map/dot_general | solution.py:52
  266.6 0.0 all-reduce.4.cloned.1.call-update
  266.6 11.5 %all-to-all-done.2 = bf16[128,8,4,256]{0,2,1,3:T(4,128)(2,1)S(1)} async-done(((bf16[128,8,4,256]{0,2,1,3:T(4,128)(2,1)}), bf16[128,8,4,256]{0,2,1,3:T(4,128)(2,1)S(1)}, u32[]{:S(2)}, u32[]{:S(2)}) %all-to-all-start.2) | async-done | bytes 2097184 | tf_op jit(solution)/shard_map/all_to_all | solution.py:161
  278.1 0.8 copy.110
  278.9 2.0 copy.111
  280.8 2.5 reshape.299
  283.3 2.9 convert_bitcast_fusion
  286.2 1.2 copy.112
  287.4 3.2 copy.113
  290.6 8.0 %all-to-all-start.3 = ((bf16[192,8,4,128]{3,1,2,0:T(8,128)(2,1)}), bf16[192,8,4,128]{3,1,2,0:T(8,128)(2,1)S(1)}, u32[]{:S(2)}, u32[]{:S(2)}) async-start(bf16[192,8,4,128]{3,1,2,0:T(8,128)(2,1)} %copy.113), calls=%async_computation.3 | async-start | bytes 3145728 | tf_op jit(solution)/shard_map/all_to_all | solution.py:163
  298.6 76.6 %all-reduce = (f32[256]{0:T(256)S(1)}, f32[512]{0:T(512)S(1)}, f32[512]{0:T(512)S(1)}) all-reduce(f32[256]{0:T(256)S(1)} %get-tuple-element.49, f32[512]{0:T(512)S(1)} %get-tuple-element.70, f32[512]{0:T(512)S(1)} %get-tuple-element.72), channel_id=1, replica_groups=mesh['lat'=32,'lev'=4] {'lat','lev'}, use_global_device_ids=true, to_apply=%region_3.4 | all-reduce | flops 1280 | bytes 10240 | tf_op jit(solution)/shard_map/psum | solution.py:164
  375.3 0.6 broadcast_multiply_fusion.7
  375.8 0.6 broadcast_multiply_fusion.5
  376.4 49.5 %all-reduce.4.cloned.1.call-done = (f32[256,512]{1,0:T(8,128)}, f32[512,512]{1,0:T(8,128)}, f32[512,256]{1,0:T(8,128)}) async-done(((f32[256,512]{1,0:T(8,128)}, f32[512,512]{1,0:T(8,128)}, f32[512,256]{1,0:T(8,128)}), (f32[256,512]{1,0:T(8,128)}, f32[512,512]{1,0:T(8,128)}, f32[512,256]{1,0:T(8,128)})) %all-reduce.4.cloned.1.call-update) | async-done | bytes 2097168 | tf_op jit(solution)/shard_map/psum | solution.py:164
  425.9 1.9 broadcast_multiply_fusion.2
  427.8 1.9 broadcast_multiply_fusion.1
  429.7 2.3 broadcast_multiply_fusion
  432.0 1.9 fusion.1
  433.9 2.1 copy.115
  (40 shorter events, 0.1 us)
Async XLA Ops:
  7.2 1.6 copy-start
  8.1 2.6 copy-start.12
  17.2 12.1 %copy-start.15 = (s32[192]{0:T(256)S(1)}, s32[192]{0:T(256)}, u32[]{:S(2)}) copy-start(s32[192]{0:T(256)} %param.15) | copy-start | bytes 2308
  17.2 52.7 %all-to-all-start = ((bf16[6,256,8,128]{3,2,0,1:T(8,128)(2,1)}), bf16[6,256,8,128]{3,2,0,1:T(8,128)(2,1)}, u32[]{:S(2)}, u32[]{:S(2)}) async-start(bf16[6,256,8,128]{3,2,0,1:T(8,128)(2,1)} %copy.95), calls=%async_computation | async-start | bytes 6291456 | tf_op jit(solution)/shard_map/all_to_all | solution.py:23
  84.4 3.7 copy-start.6
  205.8 19.1 %copy-start.7 = (bf16[4096,256]{1,0:T(8,128)(2,1)}, bf16[4096,256]{1,0:T(8,128)(2,1)S(1)}, u32[]{:S(2)}) copy-start(bf16[4096,256]{1,0:T(8,128)(2,1)S(1)} %reshape.291) | copy-start | bytes 6291460
  212.1 5.4 %copy-start.10 = (bf16[256,512]{1,0:T(8,128)(2,1)S(1)}, bf16[256,512]{1,0:T(8,128)(2,1)}, u32[]{:S(2)}) copy-start(bf16[256,512]{1,0:T(8,128)(2,1)} %param.17) | copy-start | bytes 786436
  212.1 5.4 %copy-start.14 = (f32[256]{0:T(256)S(1)}, f32[256]{0:T(256)}, u32[]{:S(2)}) copy-start(f32[256]{0:T(256)} %param.16) | copy-start | bytes 3076
  212.1 5.4 %copy-start.17 = (f32[512]{0:T(512)S(1)}, f32[512]{0:T(512)}, u32[]{:S(2)}) copy-start(f32[512]{0:T(512)} %param.18) | copy-start | bytes 6148
  217.5 4.9 %copy-start.9 = (bf16[512,512]{1,0:T(8,128)(2,1)S(1)}, bf16[512,512]{1,0:T(8,128)(2,1)}, u32[]{:S(2)}) copy-start(bf16[512,512]{1,0:T(8,128)(2,1)} %param.19) | copy-start | bytes 1572868
  222.4 2.5 copy-start.16
  222.4 2.5 copy-start.18
  224.9 3.9 copy-start.4
  232.1 4.5 %copy-start.2 = (f32[4096,256]{1,0:T(8,128)S(1)}, f32[4096,256]{1,0:T(8,128)}, u32[]{:S(2)}) copy-start(f32[4096,256]{1,0:T(8,128)} %reshape.294) | copy-start | bytes 12582916
  236.6 1.9 copy-start.3
  248.4 29.7 %all-to-all-start.2 = ((bf16[128,8,4,256]{0,2,1,3:T(4,128)(2,1)}), bf16[128,8,4,256]{0,2,1,3:T(4,128)(2,1)S(1)}, u32[]{:S(2)}, u32[]{:S(2)}) async-start(bf16[128,8,4,256]{0,2,1,3:T(4,128)(2,1)} %copy.109), calls=%async_computation.2 | async-start | bytes 4194304 | tf_op jit(solution)/shard_map/all_to_all | solution.py:161
  253.0 172.9 %all-reduce.4.cloned.1.call-start = ((), (), s32[]{:S(2)}) async-start(), calls=%async_computation.4 | async-start | bytes 4194304 | tf_op jit(solution)/shard_map/psum | solution.py:164
  253.0 6.9 %copy-start.8 = (bf16[4096,256]{1,0:T(8,128)(2,1)S(1)}, bf16[4096,256]{1,0:T(8,128)(2,1)}, u32[]{:S(2)}) copy-start(bf16[4096,256]{1,0:T(8,128)(2,1)} %copy-done.7) | copy-start | bytes 6291460
  290.6 141.4 %copy-start.5 = (bf16[6,171,256]{2,1,0:T(8,128)(2,1)S(1)}, bf16[6,171,256]{2,1,0:T(8,128)(2,1)}, u32[]{:S(2)}) copy-start(bf16[6,171,256]{2,1,0:T(8,128)(2,1)} %param.13) | copy-start | bytes 1575940
  290.6 141.4 %copy-start.11 = (f32[6,171]{1,0:T(8,128)S(1)}, f32[6,171]{1,0:T(8,128)}, u32[]{:S(2)}) copy-start(f32[6,171]{1,0:T(8,128)} %get-tuple-element.63) | copy-start | bytes 12316
  290.6 141.4 %copy-start.13 = (pred[6,171]{1,0:T(8,128)(4,1)S(1)}, pred[6,171]{1,0:T(8,128)(4,1)}, u32[]{:S(2)}) copy-start(pred[6,171]{1,0:T(8,128)(4,1)} %copy-done.12) | copy-start | bytes 3082
  290.6 141.4 %all-to-all-start.3 = ((bf16[192,8,4,128]{3,1,2,0:T(8,128)(2,1)}), bf16[192,8,4,128]{3,1,2,0:T(8,128)(2,1)S(1)}, u32[]{:S(2)}, u32[]{:S(2)}) async-start(bf16[192,8,4,128]{3,1,2,0:T(8,128)(2,1)} %copy.113), calls=%async_computation.3 | async-start | bytes 3145728 | tf_op jit(solution)/shard_map/all_to_all | solution.py:163
  432.0 4.1 copy-start.1
Sparse Core Ops, SparseCore 0:
  266.7 159.1 all-reduce.3
where the time goes:
time: 449 us; the launch traced here: 443 us
  blocking collectives  132 us (29%)
  local copies, waits for them, and re-layouts  99.7 us (22%)
  waiting for transfers between devices  99.7 us (22%)
  matrix products  49.4 us (11%)
  starting transfers between devices  24.8 us (6%)
  other arithmetic  23.3 us (5%)
  between operations  14.6 us (3%)
    psum x1, blocking collectives, local(): lax.psum((grads_local[0], grads_local[1], grads_local[2], grads_local[3],...  76.6 us
    all_to_all x1, blocking collectives, in_one_piece(): lax.all_to_all(both, axis, split_axis=split_dim, concat_axis=concat_dim,...  55.2 us
    psum x1, waiting for transfers between devices, local(): lax.psum((grads_local[0], grads_local[1], grads_local[2], grads_local[3],...  49.5 us
    all_to_all x1, waiting for transfers between devices, in_one_piece(): lax.all_to_all(both, axis, split_axis=split_dim, concat_axis=concat_dim,...  38.7 us
    unnamed x41, local copies, waits for them, and re-layouts  21.1 us
    concatenate x2, local copies, waits for them, and re-layouts, in_one_piece(): both = jnp.concatenate(arrays, axis=along)  17.5 us
    dot_general x3, matrix products, contract_rows(): lax.dot_general(left, right, (((0,), (0,)), ((), ())), preferred_element_...  16.9 us
    all_to_all x2, local copies, waits for them, and re-layouts, in_one_piece(): lax.all_to_all(both, axis, split_axis=split_dim, concat_axis=concat_dim,...  15.5 us
  transfers between devices with their start and end apart: 4, of which 3 were waited for; matrix products, arithmetic and copies ran while one was open for 8% of the time, Pallas kernels for 0%

commit v1 on v0

--- a/solution.py
+++ b/solution.py
@@ -162,15 +162,18 @@
     back_fourier = analyze(wave_table, grad_part)
     back_slots = lax.all_to_all(back_fourier, "lat", split_axis=0, concat_axis=1, tiled=True)
     summed = lax.psum(
-        (
-            grads_local[0],
-            grads_local[1],
-            grads_local[2],
-            grads_local[3],
-            grads_local[4],
-            grads_local[5],
+        lax.psum(
+            (
+                grads_local[0],
+                grads_local[1],
+                grads_local[2],
+                grads_local[3],
+                grads_local[4],
+                grads_local[5],
+            ),
+            "lev",
         ),
-        ("lat", "lev"),
+        "lat",
     )
     factor = float(MEMBERS * NLAT * NLON) ** (-0.5)
     grads = tuple((piece * factor for piece in summed))

time: 449 us -> 708 us (1.58)
  the two profiles are of different devices: /device:TPU:1 before, /device:TPU:4 now
where the time goes in v1:
time: 708 us; the launch traced here: 702 us
  waiting for transfers between devices  282 us (40%)
  blocking collectives  211 us (30%)
  local copies, waits for them, and re-layouts  100 us (14%)
  matrix products  47.7 us (7%)
  other arithmetic  25.1 us (4%)
  starting transfers between devices  21.8 us (3%)
  between operations  14.6 us (2%)
    psum x1, waiting for transfers between devices, local(): lax.psum(lax.psum((grads_local[0], grads_local[1], grads_local[2], grads_...  229 us
    psum x1, blocking collectives, local(): lax.psum(lax.psum((grads_local[0], grads_local[1], grads_local[2], grads_...  92.7 us
    all_to_all x1, blocking collectives, in_one_piece(): lax.all_to_all(both, axis, split_axis=split_dim, concat_axis=concat_dim,...  54 us
    all_to_all x1, blocking collectives, local(): lax.all_to_all(grad_grid, 'lev', split_axis=3, concat_axis=0, tiled=True)  38.5 us
    all_to_all x1, waiting for transfers between devices, in_one_piece(): lax.all_to_all(both, axis, split_axis=split_dim, concat_axis=concat_dim,...  38.4 us
    psum x1, blocking collectives, local(): lax.psum((grads_local[0], grads_local[1], grads_local[2], grads_local[3],...  25.4 us
    unnamed x33, local copies, waits for them, and re-layouts  23 us
    concatenate x2, local copies, waits for them, and re-layouts, in_one_piece(): both = jnp.concatenate(arrays, axis=along)  17.5 us
  transfers between devices with their start and end apart: 4, of which 3 were waited for; matrix products, arithmetic and copies ran while one was open for 4% of the time, Pallas kernels for 0%

profile of v1, /device:TPU:4, one launch (start us, length us, event | category | flops | bytes accessed | tf_op | source)
XLA Modules:
  0.0 701.9 jit_solution(9368156778170796093)
XLA Ops:
  7.2 0.8 broadcast_compare_fusion
  8.0 0.1 fusion.29
  8.1 0.7 broadcast_select_fusion.4
  8.8 1.9 convolution_convert_fusion
  10.7 2.4 multiply_convert_fusion.6
  13.2 0.3 pad_maximum_fusion.1
  13.5 3.7 copy.95
  17.2 11.2 %all-to-all-start = ((bf16[6,256,8,128]{3,2,0,1:T(8,128)(2,1)}), bf16[6,256,8,128]{3,2,0,1:T(8,128)(2,1)}, u32[]{:S(2)}, u32[]{:S(2)}) async-start(bf16[6,256,8,128]{3,2,0,1:T(8,128)(2,1)} %copy.95), calls=%async_computation | async-start | bytes 6291456 | tf_op jit(solution)/shard_map/all_to_all | solution.py:23
  28.4 0.5 all-reduce.9.cloned.1.call-start
  28.9 1.9 multiply_convert_fusion.8
  30.9 38.4 %all-to-all-done = bf16[6,256,8,128]{3,2,0,1:T(8,128)(2,1)} async-done(((bf16[6,256,8,128]{3,2,0,1:T(8,128)(2,1)}), bf16[6,256,8,128]{3,2,0,1:T(8,128)(2,1)}, u32[]{:S(2)}, u32[]{:S(2)}) %all-to-all-start) | async-done | bytes 3145760 | tf_op jit(solution)/shard_map/all_to_all | solution.py:23
  69.3 2.7 copy.97
  72.0 2.2 fusion.45
  74.2 5.3 copy.98
  79.6 4.2 copy.100
  83.8 3.7 bitcast_convert_fusion.1
  87.6 2.1 bitcast_convert_fusion
  89.6 2.3 pad_maximum_fusion
  91.9 13.8 %copy.102 = bf16[512,16,4,64]{3,2,1,0:T(4,128)(2,1)} copy(bf16[512,16,4,64]{0,3,2,1:T(8,128)(2,1)} %pad_maximum_fusion) | data formatting | bytes 8388608 | tf_op jit(solution)/shard_map/concatenate | solution.py:20
  105.7 9.5 %reshape.301 = bf16[4,2,262144]{2,1,0:T(2,128)(2,1)} reshape(bf16[512,16,4,64]{3,2,1,0:T(4,128)(2,1)} %copy.102) | data formatting | bytes 8388608
  115.2 54.0 %all_to_all.72 = bf16[4,2,262144]{2,1,0:T(2,128)(2,1)} all-to-all(bf16[4,2,262144]{2,1,0:T(2,128)(2,1)} %reshape.301), channel_id=1, replica_groups=mesh['lat'=32,'lev'=4] {'lev'}, dimensions={0} | all-to-all | bytes 8388608 | tf_op jit(solution)/shard_map/all_to_all | solution.py:23
  169.3 9.3 %reshape.302 = bf16[512,16,4,64]{3,2,1,0:T(4,128)(2,1)} reshape(bf16[4,2,262144]{2,1,0:T(2,128)(2,1)} %all_to_all.72) | data formatting | bytes 8388608
  178.5 12.7 %copy.104 = bf16[128,16,4,4,64]{0,4,3,2,1:T(8,128)(2,1)} copy(bf16[128,16,4,4,64]{4,2,1,0,3:T(4,128)(2,1)} %bitcast.65) | data formatting | bytes 8388608 | tf_op jit(solution)/shard_map/all_to_all | solution.py:23
  191.3 2.0 multiply_reduce_fusion.2
  193.3 4.7 fusion.44
  198.0 0.3 copy.106
  198.3 0.3 rsqrt.12
  198.6 2.9 copy.107
  201.4 2.5 reshape.291
  204.0 5.5 copy.108
  209.5 5.3 reshape.294
  214.9 4.9 multiply_convert_fusion.3
  219.8 2.4 fusion.46
  222.2 3.4 fusion
  225.6 3.8 convert_reduce_fusion
  229.5 3.3 fusion.47
  232.8 4.5 convert_reduce_fusion.1
  237.3 2.0 copy-done.3
  239.3 3.3 fusion.42
  242.6 6.9 multiply_reduce_fusion
  249.5 0.0 all-reduce.9.cloned.1.call-update
  249.5 0.0 all-reduce.7.cloned.1.call-start
  249.6 5.1 subtract_convert_fusion
  254.6 2.5 reshape.292
  257.2 4.1 copy.109
  261.2 38.5 %all_to_all.73 = bf16[128,8,4,256]{0,2,1,3:T(4,128)(2,1)S(1)} all-to-all(bf16[128,8,4,256]{0,2,1,3:T(4,128)(2,1)} %copy.109), channel_id=1, replica_groups=mesh['lat'=32,'lev'=4] {'lev'}, dimensions={3} | all-to-all | bytes 4194304 | tf_op jit(solution)/shard_map/all_to_all | solution.py:161
  299.8 0.8 copy.110
  300.6 2.0 copy.111
  302.6 2.2 reshape.299
  304.8 14.4 %all-reduce.9.cloned.1.call-done = (f32[256,512]{1,0:T(8,128)}, f32[512,512]{1,0:T(8,128)}, f32[512,256]{1,0:T(8,128)}) async-done(((f32[256,512]{1,0:T(8,128)}, f32[512,512]{1,0:T(8,128)}, f32[512,256]{1,0:T(8,128)}), (f32[256,512]{1,0:T(8,128)}, f32[512,512]{1,0:T(8,128)}, f32[512,256]{1,0:T(8,128)})) %all-reduce.9.cloned.1.call-update) | async-done | bytes 2097168 | tf_op jit(solution)/shard_map/psum | solution.py:165
  319.2 2.9 convert_bitcast_fusion
  322.1 1.2 copy.112
  323.3 3.2 copy.113
  326.5 10.0 %all-to-all-start.3 = ((bf16[192,8,4,128]{3,1,2,0:T(8,128)(2,1)}), bf16[192,8,4,128]{3,1,2,0:T(8,128)(2,1)S(1)}, u32[]{:S(2)}, u32[]{:S(2)}) async-start(bf16[192,8,4,128]{3,1,2,0:T(8,128)(2,1)} %copy.113), calls=%async_computation.3 | async-start | bytes 3145728 | tf_op jit(solution)/shard_map/all_to_all | solution.py:163
  336.5 25.4 %all-reduce.2 = (f32[256]{0:T(256)S(1)}, f32[512]{0:T(512)S(1)}, f32[512]{0:T(512)S(1)}) all-reduce(f32[256]{0:T(256)S(1)} %get-tuple-element.49, f32[512]{0:T(512)S(1)} %get-tuple-element.76, f32[512]{0:T(512)S(1)} %get-tuple-element.78), channel_id=1, replica_groups=mesh['lat'=32,'lev'=4] {'lev'}, use_global_device_ids=true, to_apply=%region_3.4 | all-reduce | flops 1280 | bytes 10240 | tf_op jit(solution)/shard_map/psum | solution.py:165
  361.9 92.7 %all-reduce = (f32[256]{0:T(256)S(1)}, f32[512]{0:T(512)S(1)}, f32[512]{0:T(512)S(1)}) all-reduce(f32[256]{0:T(256)S(1)} %get-tuple-element.57, f32[512]{0:T(512)S(1)} %get-tuple-element.58, f32[512]{0:T(512)S(1)} %get-tuple-element.59), channel_id=1, replica_groups=mesh['lat'=32,'lev'=4] {'lat'}, use_global_device_ids=true, to_apply=%region_4.5 | all-reduce | flops 1280 | bytes 10240 | tf_op jit(solution)/shard_map/psum | solution.py:164
  454.6 0.6 broadcast_multiply_fusion.7
  455.2 0.6 broadcast_multiply_fusion.5
  455.8 2.0 fusion.1
  457.8 2.1 copy.115
  460.0 228.8 %all-reduce.7.cloned.1.call-done = (f32[256,512]{1,0:T(8,128)}, f32[512,512]{1,0:T(8,128)}, f32[512,256]{1,0:T(8,128)}) async-done(((f32[256,512]{1,0:T(8,128)}, f32[512,512]{1,0:T(8,128)}, f32[512,256]{1,0:T(8,128)}), (f32[256,512]{1,0:T(8,128)}, f32[512,512]{1,0:T(8,128)}, f32[512,256]{1,0:T(8,128)})) %all-reduce.7.cloned.1.call-update) | async-done | bytes 2097168 | tf_op jit(solution)/shard_map/psum | solution.py:164
  688.7 1.9 broadcast_multiply_fusion.2
  690.6 1.9 broadcast_multiply_fusion.1
  692.5 2.3 broadcast_multiply_fusion
  (35 shorter events, 0.1 us)
Async XLA Ops:
  7.2 1.6 copy-start
  8.1 2.6 copy-start.8
  17.2 11.8 %copy-start.11 = (s32[192]{0:T(256)S(1)}, s32[192]{0:T(256)}, u32[]{:S(2)}) copy-start(s32[192]{0:T(256)} %param.15) | copy-start | bytes 2308
  17.2 52.1 %all-to-all-start = ((bf16[6,256,8,128]{3,2,0,1:T(8,128)(2,1)}), bf16[6,256,8,128]{3,2,0,1:T(8,128)(2,1)}, u32[]{:S(2)}, u32[]{:S(2)}) async-start(bf16[6,256,8,128]{3,2,0,1:T(8,128)(2,1)} %copy.95), calls=%async_computation | async-start | bytes 6291456 | tf_op jit(solution)/shard_map/all_to_all | solution.py:23
  28.4 290.8 %all-reduce.9.cloned.1.call-start = ((), (), s32[]{:S(2)}) async-start(), calls=%async_computation.5 | async-start | bytes 4194304 | tf_op jit(solution)/shard_map/psum | solution.py:165
  83.8 3.7 copy-start.4
  209.5 5.3 copy-start.6
  209.5 5.3 copy-start.10
  209.5 5.3 copy-start.14
  214.8 4.9 copy-start.5
  219.8 2.4 copy-start.13
  222.2 3.4 copy-start.12
  232.8 6.4 copy-start.2
  237.3 2.0 copy-start.3
  249.5 439.2 %all-reduce.7.cloned.1.call-start = ((), (), s32[]{:S(2)}) async-start(), calls=%async_computation.4 | async-start | bytes 4194304 | tf_op jit(solution)/shard_map/psum | solution.py:164
  323.3 132.4 %copy-start.7 = (f32[6,171]{1,0:T(8,128)S(1)}, f32[6,171]{1,0:T(8,128)}, u32[]{:S(2)}) copy-start(f32[6,171]{1,0:T(8,128)} %get-tuple-element.69) | copy-start | bytes 12316
  323.3 132.4 %copy-start.9 = (pred[6,171]{1,0:T(8,128)(4,1)S(1)}, pred[6,171]{1,0:T(8,128)(4,1)}, u32[]{:S(2)}) copy-start(pred[6,171]{1,0:T(8,128)(4,1)} %copy-done.8) | copy-start | bytes 3082
  326.5 129.2 %all-to-all-start.3 = ((bf16[192,8,4,128]{3,1,2,0:T(8,128)(2,1)}), bf16[192,8,4,128]{3,1,2,0:T(8,128)(2,1)S(1)}, u32[]{:S(2)}, u32[]{:S(2)}) async-start(bf16[192,8,4,128]{3,1,2,0:T(8,128)(2,1)} %copy.113), calls=%async_computation.3 | async-start | bytes 3145728 | tf_op jit(solution)/shard_map/all_to_all | solution.py:163
  455.8 239.0 %copy-start.1 = (bf16[6,171,4,128]{3,2,1,0:T(4,128)(2,1)S(1)}, bf16[6,171,4,128]{3,2,1,0:T(4,128)(2,1)}, u32[]{:S(2)}) copy-start(bf16[6,171,4,128]{3,2,1,0:T(4,128)(2,1)} %param.11) | copy-start | bytes 3151876
Sparse Core Ops, SparseCore 0:
  249.6 69.5 all-reduce.8
  321.9 366.7 all-reduce.6
